TPU v7x, 512 devices: a 8x2x16 block of a 8x8x16 slice. The times are simulated.
512 devices in a mesh: rep: 2 (over y), exp: 16 (over x, core), tp: 16 (over z).
Axes of the slice: x: 8, y: 2, z: 16, core: 2. Of those that a mesh axis runs over, the one named last changes fastest.
The devices are a block of a 8x8x16 slice.
Arguments:
- tokens: bfloat16 [1024, 6144], P(('rep', 'exp'), 'tp'), parts along dimension 0, may hold values from -6 to 6
- expert_ids: int32 [1024, 2], P(('rep', 'exp')), parts along dimension 0, may hold values from 0 to 3, all different within a row; in each aligned block of 32 rows (0 to 31, 32 to 63, ...) at most 20 rows name the same one
- route_logits: float32 [1024, 2], P(('rep', 'exp')), parts along dimension 0, may hold values from -6 to 6
- gate_weight: bfloat16 [6144, 32768], P(None, ('exp', 'tp')), may hold values from -0.078125 to 0.078125
- up_weight: bfloat16 [6144, 32768], P(None, ('exp', 'tp')), may hold values from -0.078125 to 0.078125
- down_weight: bfloat16 [32768, 6144], P(('exp', 'tp')), may hold values from -0.0625 to 0.0625
Outputs:
- moe_out: bfloat16 [1024, 6144], P(('rep', 'exp'), 'tp'), parts along dimension 0
There are 2 independent parts, one for each index of `rep`. A program takes and returns all parts, laid end to end along the dimension named above; an argument that names none is the same for every part. Nothing has to cross between parts.
Inputs may be any that keep to these rules, and one draw needn't show every extreme that they name: `expert_ids`: each token names two different experts. In each aligned block of 32 tokens no expert is named by more than 20 tokens, a bound that some block reaches.
All inputs are finite; a program needn't handle non-finite values.
Results may differ from a plain program's by a relative error of at most 0.019.
Values may be sent and summed in bfloat16 or wider, within the bound.
No kernel may reach another device: no remote copies, remote signals or barrier semaphores. Data moves between devices by JAX's collectives and lax.ppermute only.
A program may use at most 64 MiB of HBM per device.

v0:
```python
import jax
import jax.numpy as jnp
from jax import lax
from jax.sharding import PartitionSpec as P

D = 6144
EXPERTS = 4
CAP = 20


def cut_along(x, dim, devices):
    shape = x.shape
    blocks = x.reshape(*shape[:dim], devices, shape[dim] // devices, *shape[dim + 1 :])
    return jnp.moveaxis(blocks, dim, 0)


def sum_at_owner(x, axis, dim):
    devices = lax.axis_size(axis)
    blocks = lax.all_to_all(cut_along(x, dim, devices), axis, 0, 0, tiled=True)
    return jnp.sum(blocks.astype(jnp.float32), axis=0)


def slot_tables(expert_ids, route_logits):
    chosen = (expert_ids[:, :, None] == jnp.arange(EXPERTS, dtype=jnp.int32)[None, None, :]).astype(
        jnp.int32
    )
    per_token = jnp.sum(chosen, axis=1)
    before = jnp.cumsum(per_token, axis=0) - per_token
    position = jnp.sum(chosen * before[:, None, :], axis=2)
    at_slot = (position[:, :, None] == jnp.arange(CAP, dtype=jnp.int32)[None, None, :]).astype(
        jnp.float32
    )
    chosen_f = chosen.astype(jnp.float32)
    diff = route_logits[:, 0] - route_logits[:, 1]
    shares = jnp.stack([jax.nn.sigmoid(diff), jax.nn.sigmoid(-diff)], axis=1)
    placement = jnp.einsum("tke,tkc->ect", chosen_f, at_slot)
    mixing = jnp.einsum("tk,tke,tkc->tec", shares, chosen_f, at_slot)
    return (placement.astype(jnp.bfloat16), mixing)


def on_device(tokens, expert_ids, route_logits, gate_weight, up_weight, down_weight):
    exp_count = lax.axis_size("exp")
    groups = exp_count // EXPERTS
    placement, mixing = slot_tables(expert_ids, route_logits)
    slots = jnp.einsum("ect,td->ecd", placement, tokens, preferred_element_type=jnp.float32).astype(
        jnp.bfloat16
    )
    outgoing = jnp.repeat(slots, groups, axis=0)
    incoming = lax.all_to_all(outgoing, "exp", split_axis=0, concat_axis=0, tiled=True)
    gathered = lax.all_gather(incoming, "tp", axis=2, tiled=True)
    slot_rows = gathered.reshape(exp_count * CAP, D)
    gate_act = jnp.dot(slot_rows, gate_weight, preferred_element_type=jnp.float32)
    up_act = jnp.dot(slot_rows, up_weight, preferred_element_type=jnp.float32)
    hidden = (jax.nn.silu(gate_act) * up_act).astype(jnp.bfloat16)
    partial_value = jnp.dot(hidden, down_weight, preferred_element_type=jnp.float32).astype(
        jnp.bfloat16
    )
    partial_value = lax.optimization_barrier(partial_value).reshape(exp_count, CAP, D)
    returned = lax.all_to_all(partial_value, "exp", split_axis=0, concat_axis=0, tiled=True)
    summed = jnp.sum(returned.astype(jnp.float32).reshape(EXPERTS, groups, CAP, D), axis=1)
    combined = jnp.einsum("tec,ecd->td", mixing, summed)
    moe_out = sum_at_owner(combined.astype(jnp.bfloat16), "tp", 1).astype(jnp.bfloat16)
    return moe_out


def solution(mesh):
    return jax.shard_map(
        on_device,
        mesh=mesh,
        in_specs=(
            P(("rep", "exp"), "tp"),
            P(("rep", "exp"), None),
            P(("rep", "exp"), None),
            P(None, ("exp", "tp")),
            P(None, ("exp", "tp")),
            P(("exp", "tp"), None),
        ),
        out_specs=P(("rep", "exp"), "tp"),
        check_vma=False,
    )
```

profile of v0, /device:TPU:70, one launch (start us, length us, event | category | flops | bytes accessed | tf_op | source)
XLA Modules:
  0.0 322.3 jit_solution(2993547651281507378)
XLA Ops:
  6.5 0.0 copy-start
  6.6 0.0 all-gather.2.cloned.1.call-start
  6.6 0.9 copy.12
  7.4 0.1 convert_reduce_fusion.1
  7.6 0.1 reduce_window_sum.11
  7.6 0.7 select_reduce_fusion
  8.3 0.4 fusion.2
  8.7 0.9 convolution_convert_fusion.1
  9.7 53.4 %all_to_all.15 = bf16[16,20,384]{2,1,0:T(8,128)(2,1)} all-to-all(bf16[16,20,384]{2,1,0:T(8,128)(2,1)S(1)} %bitcast.28), channel_id=1, replica_groups=mesh['rep'=2,'exp'=16,'tp'=16] {'exp'}, dimensions={0} | all-to-all | bytes 491520 | tf_op jit(solution)/shard_map/all_to_all | solution.py:49
  63.0 0.1 all-gather.2.cloned.1.call-update
  63.1 0.0 copy-start.1
  63.1 78.8 %all-gather.2.cloned.1.call-done = bf16[16,20,6144]{2,1,0:T(8,128)(2,1)} async-done(((bf16[16,20,384]{2,1,0:T(8,128)(2,1)}), bf16[16,20,6144]{2,1,0:T(8,128)(2,1)}) %all-gather.2.cloned.1.call-update) | async-done | bytes 3932176 | tf_op jit(solution)/shard_map/all_gather | solution.py:50
  141.9 7.0 %reshape.30 = bf16[320,6144]{1,0:T(8,128)(2,1)} reshape(bf16[16,20,6144]{2,1,0:T(8,128)(2,1)} %all-gather.2.cloned.1.call-done) | data formatting | bytes 7864320 | tf_op jit(solution)/shard_map/reshape | solution.py:51
  148.8 0.0 copy-done.1
  148.8 3.3 %fusion.21 = f32[320,128]{1,0:T(8,128)S(1)} fusion(bf16[320,6144]{1,0:T(8,128)(2,1)} %reshape.30, bf16[6144,128]{1,0:T(8,128)(2,1)S(1)} %copy-done.1), kind=kOutput, calls=%fused_computation.36 | convolution fusion | flops 503316480 | bytes 5668864 | tf_op jit(solution)/shard_map/dot_general | solution.py:52
  152.1 0.0 copy-done
  152.1 8.7 %convolution_convert_fusion = bf16[320,6144]{1,0:T(8,128)(2,1)} fusion(bf16[128,6144]{1,0:T(8,128)(2,1)S(1)} %copy-done, bf16[320,6144]{1,0:T(8,128)(2,1)} %reshape.30, bf16[6144,128]{1,0:T(8,128)(2,1)} %param.10, f32[320,128]{1,0:T(8,128)S(1)} %fusion.21), kind=kOutput, calls=%fused_computation.1 | convolution fusion | flops 1008844800 | bytes 11173888 | tf_op jit(solution)/shard_map/dot_general | solution.py:55
  160.9 6.9 %reshape.31 = bf16[16,20,6144]{2,1,0:T(8,128)(2,1)} reshape(bf16[320,6144]{1,0:T(8,128)(2,1)} %convolution_convert_fusion) | data formatting | bytes 7864320 | tf_op jit(solution)/shard_map/reshape | solution.py:58
  167.7 0.0 copy-start.2
  167.7 7.4 %all-to-all-start.1 = ((bf16[16,20,6144]{2,1,0:T(8,128)(2,1)}), bf16[16,20,6144]{2,1,0:T(8,128)(2,1)}, u32[]{:S(2)}, u32[]{:S(2)}) async-start(bf16[16,20,6144]{2,1,0:T(8,128)(2,1)} %reshape.31), calls=%async_computation.1 | async-start | bytes 9437184 | tf_op jit(solution)/shard_map/all_to_all | solution.py:59
  175.1 0.0 copy-done.2
  175.2 0.1 copy.11
  175.3 0.4 fusion.11
  175.7 104.4 %all-to-all-done.1 = bf16[16,20,6144]{2,1,0:T(8,128)(2,1)} async-done(((bf16[16,20,6144]{2,1,0:T(8,128)(2,1)}), bf16[16,20,6144]{2,1,0:T(8,128)(2,1)}, u32[]{:S(2)}, u32[]{:S(2)}) %all-to-all-start.1) | async-done | bytes 3932192 | tf_op jit(solution)/shard_map/all_to_all | solution.py:59
  280.1 3.2 convert_reduce_fusion
  283.3 0.5 fusion
  283.8 0.1 copy.22
  283.9 30.8 %all_to_all.16 = bf16[16,32,384]{2,1,0:T(8,128)(2,1)S(1)} all-to-all(bf16[16,32,384]{2,1,0:T(8,128)(2,1)S(1)} %bitcast.26), channel_id=1, replica_groups=mesh['rep'=2,'exp'=16,'tp'=16] {'tp'}, dimensions={0} | all-to-all | bytes 786432 | tf_op jit(solution)/shard_map/all_to_all | solution.py:19
  314.7 0.7 reduce_sum.42
  (4 shorter events, 0.1 us)
Async XLA Ops:
  6.5 145.6 %copy-start = (bf16[128,6144]{1,0:T(8,128)(2,1)S(1)}, bf16[128,6144]{1,0:T(8,128)(2,1)}, u32[]{:S(2)}) copy-start(bf16[128,6144]{1,0:T(8,128)(2,1)} %param.11) | copy-start | bytes 4718596
  6.6 135.3 %all-gather.2.cloned.1.call-start = ((), (), s32[]{:S(2)}) async-start(), calls=%async_computation.3 | async-start | bytes 5013504 | tf_op jit(solution)/shard_map/all_gather | solution.py:50
  63.1 85.8 %copy-start.1 = (bf16[6144,128]{1,0:T(8,128)(2,1)S(1)}, bf16[6144,128]{1,0:T(8,128)(2,1)}, u32[]{:S(2)}) copy-start(bf16[6144,128]{1,0:T(8,128)(2,1)} %param.9) | copy-start | bytes 4718596
  167.7 7.4 %copy-start.2 = (f32[32,2]{0,1:T(2,128)S(1)}, f32[32,2]{0,1:T(2,128)}, u32[]{:S(2)}) copy-start(f32[32,2]{0,1:T(2,128)} %param.8) | copy-start | bytes 772
  167.7 112.3 %all-to-all-start.1 = ((bf16[16,20,6144]{2,1,0:T(8,128)(2,1)}), bf16[16,20,6144]{2,1,0:T(8,128)(2,1)}, u32[]{:S(2)}, u32[]{:S(2)}) async-start(bf16[16,20,6144]{2,1,0:T(8,128)(2,1)} %reshape.31), calls=%async_computation.1 | async-start | bytes 9437184 | tf_op jit(solution)/shard_map/all_to_all | solution.py:59
Sparse Core Ops, SparseCore 0:
  63.2 78.6 all-gather.1
where the time goes:
time: 323 us; the launch traced here: 322 us
  waiting for transfers between devices  183 us (57%)
  blocking collectives  84.2 us (26%)
  local copies, waits for them, and re-layouts  14.9 us (5%)
  matrix products  14.3 us (4%)
  between operations  13.5 us (4%)
  starting transfers between devices  7.38 us (2%)
  other arithmetic  4.76 us (1%)
    all_to_all x1, waiting for transfers between devices, on_device(): lax.all_to_all(partial_value, 'exp', split_axis=0, concat_axis=0, tiled=T...  104 us
    all_gather x1, waiting for transfers between devices, on_device(): gathered = lax.all_gather(incoming, 'tp', axis=2, tiled=True)  78.8 us
    all_to_all x1, blocking collectives, on_device(): lax.all_to_all(outgoing, 'exp', split_axis=0, concat_axis=0, tiled=True)  53.4 us
    all_to_all x1, blocking collectives, sum_at_owner(): blocks = lax.all_to_all(cut_along(x, dim, devices), axis, 0, 0, tiled=True)  30.8 us
    dot_general x1, matrix products, on_device(): jnp.dot(hidden, down_weight, preferred_element_type=jnp.float32)  8.73 us
    all_to_all x1, starting transfers between devices, on_device(): lax.all_to_all(partial_value, 'exp', split_axis=0, concat_axis=0, tiled=T...  7.38 us
    reshape x1, local copies, waits for them, and re-layouts, on_device(): slot_rows = gathered.reshape(exp_count * CAP, D)  6.97 us
    reshape x1, local copies, waits for them, and re-layouts, on_device(): lax.optimization_barrier(partial_value).reshape(exp_count, CAP, D)  6.87 us
  transfers between devices with their start and end apart: 2, of which 2 were waited for; matrix products, arithmetic and copies ran while one was open for 0% of the time, Pallas kernels for 0%

commit v1 on v0

--- a/solution.py
+++ b/solution.py
@@ -47,7 +47,16 @@
     )
     outgoing = jnp.repeat(slots, groups, axis=0)
     incoming = lax.all_to_all(outgoing, "exp", split_axis=0, concat_axis=0, tiled=True)
-    gathered = lax.all_gather(incoming, "tp", axis=2, tiled=True)
+    form_point_on = lambda buf, which_axis: jnp.concatenate(
+        jax.lax.all_to_all(
+            jnp.stack([buf] * jax.lax.axis_size(which_axis), axis=0),
+            split_axis=0,
+            axis_name=which_axis,
+            concat_axis=0,
+        ),
+        axis=2,
+    )
+    gathered = form_point_on(incoming, "tp")
     slot_rows = gathered.reshape(exp_count * CAP, D)
     gate_act = jnp.dot(slot_rows, gate_weight, preferred_element_type=jnp.float32)
     up_act = jnp.dot(slot_rows, up_weight, preferred_element_type=jnp.float32)

time: 323 us -> 409 us (1.27)
  blocking collectives: 84.2 us -> 267 us
  waiting for transfers between devices: 183 us -> 104 us
  between operations: 13.5 us -> 0.12 us
    all_to_all x0 -> x1, blocking collectives: none -> 184 us  [on_device(): jax.lax.all_to_all(jnp.stack([buf] * jax.lax.axis_size(which_axis), axis=...]
    all_gather x1 -> x0, waiting for transfers between devices: 78.8 us -> none  [on_device(): gathered = lax.all_gather(incoming, 'tp', axis=2, tiled=True)]
    reshape x1, local copies, waits for them, and re-layouts: 6.97 us -> 2.34 us  [on_device(): jnp.concatenate(jax.lax.all_to_all(jnp.stack([buf] * jax.lax.axis_size(wh...]
  transfers between devices with their start and end apart: 2 -> 1, of which waited for: 2 -> 1; matrix products, arithmetic and copies ran while one was open for 0% -> 0% of each run, Pallas kernels for 0% -> 0%
where the time goes in v1:
time: 409 us; the launch traced here: 408 us
  blocking collectives  267 us (65%)
  waiting for transfers between devices  104 us (25%)
  local copies, waits for them, and re-layouts  13.9 us (3%)
  matrix products  11.7 us (3%)
  starting transfers between devices  6.81 us (2%)
  other arithmetic  4.76 us (1%)
    all_to_all x1, blocking collectives, on_device(): jax.lax.all_to_all(jnp.stack([buf] * jax.lax.axis_size(which_axis), axis=...  184 us
    all_to_all x1, waiting for transfers between devices, on_device(): lax.all_to_all(partial_value, 'exp', split_axis=0, concat_axis=0, tiled=T...  104 us
    all_to_all x1, blocking collectives, on_device(): lax.all_to_all(outgoing, 'exp', split_axis=0, concat_axis=0, tiled=True)  52.7 us
    all_to_all x1, blocking collectives, sum_at_owner(): blocks = lax.all_to_all(cut_along(x, dim, devices), axis, 0, 0, tiled=True)  29.8 us
    dot_general x1, matrix products, on_device(): jnp.dot(hidden, down_weight, preferred_element_type=jnp.float32)  8.25 us
  transfers between devices with their start and end apart: 1, of which 1 were waited for; matrix products, arithmetic and copies ran while one was open for 0% of the time, Pallas kernels for 0%

profile of v1, /device:TPU:70, one launch (start us, length us, event | category | flops | bytes accessed | tf_op | source)
XLA Modules:
  0.0 408.4 jit_solution(4356644125129430857)
XLA Ops:
  0.0 0.0 copy-start
  0.0 0.9 copy.25
  0.9 0.1 convert_reduce_fusion.1
  1.0 0.1 reduce_window_sum.11
  1.1 0.7 select_reduce_fusion
  1.8 0.4 fusion.2
  2.1 0.9 convolution_convert_fusion.1
  3.1 52.7 %all_to_all.20 = bf16[16,20,384]{2,1,0:T(8,128)(2,1)S(1)} all-to-all(bf16[16,20,384]{2,1,0:T(8,128)(2,1)S(1)} %bitcast.36), channel_id=1, replica_groups=mesh['rep'=2,'exp'=16,'tp'=16] {'exp'}, dimensions={0} | all-to-all | bytes 491520 | tf_op jit(solution)/shard_map/all_to_all | solution.py:49
  55.8 0.5 stack.5
  56.3 184.2 %all_to_all.21 = bf16[16,16,20,384]{3,1,2,0:T(8,128)(2,1)S(1)} all-to-all(bf16[16,16,20,384]{3,1,2,0:T(8,128)(2,1)S(1)} %stack.5), channel_id=1, replica_groups=mesh['rep'=2,'exp'=16,'tp'=16] {'tp'}, dimensions={0} | all-to-all | bytes 7864320 | tf_op jit(solution)/shard_map/all_to_all | solution.py:51
  240.5 2.3 copy.28
  242.9 0.0 copy-start.2
  242.9 1.2 copy.32
  244.1 0.0 copy-start.1
  244.1 0.0 copy-start.3
  244.1 1.9 copy-done.1
  246.0 0.0 copy-done.2
  246.0 1.2 fusion.21
  247.2 0.0 copy-done
  247.2 0.0 copy-done.3
  247.2 8.3 %convolution_convert_fusion = bf16[320,6144]{1,0:T(8,128)(2,1)} fusion(bf16[128,6144]{1,0:T(8,128)(2,1)S(1)} %copy-done, bf16[320,6144]{1,0:T(8,128)(2,1)} %bitcast.31, bf16[6144,128]{1,0:T(8,128)(2,1)S(1)} %copy-done.3, f32[320,128]{1,0:T(8,128)S(1)} %fusion.21), kind=kOutput, calls=%fused_computation.1 | convolution fusion | flops 1008844800 | bytes 11173888 | tf_op jit(solution)/shard_map/dot_general | solution.py:64
  255.5 6.9 %reshape.33 = bf16[16,20,6144]{2,1,0:T(8,128)(2,1)} reshape(bf16[320,6144]{1,0:T(8,128)(2,1)} %convolution_convert_fusion) | data formatting | bytes 7864320 | tf_op jit(solution)/shard_map/reshape | solution.py:67
  262.3 6.8 %all-to-all-start.2 = ((bf16[16,20,6144]{2,1,0:T(8,128)(2,1)}), bf16[16,20,6144]{2,1,0:T(8,128)(2,1)}, u32[]{:S(2)}, u32[]{:S(2)}) async-start(bf16[16,20,6144]{2,1,0:T(8,128)(2,1)} %reshape.33), calls=%async_computation.2 | async-start | bytes 9437184 | tf_op jit(solution)/shard_map/all_to_all | solution.py:68
  269.2 0.0 copy-done.4
  269.2 0.1 copy.24
  269.3 0.4 fusion.11
  269.7 104.4 %all-to-all-done.2 = bf16[16,20,6144]{2,1,0:T(8,128)(2,1)} async-done(((bf16[16,20,6144]{2,1,0:T(8,128)(2,1)}), bf16[16,20,6144]{2,1,0:T(8,128)(2,1)}, u32[]{:S(2)}, u32[]{:S(2)}) %all-to-all-start.2) | async-done | bytes 3932192 | tf_op jit(solution)/shard_map/all_to_all | solution.py:68
  374.1 3.2 convert_reduce_fusion
  377.4 0.5 fusion
  377.9 0.1 copy.38
  377.9 29.8 %all_to_all.22 = bf16[16,32,384]{2,1,0:T(8,128)(2,1)S(1)} all-to-all(bf16[16,32,384]{2,1,0:T(8,128)(2,1)S(1)} %bitcast.34), channel_id=1, replica_groups=mesh['rep'=2,'exp'=16,'tp'=16] {'tp'}, dimensions={0} | all-to-all | bytes 786432 | tf_op jit(solution)/shard_map/all_to_all | solution.py:19
  407.8 0.7 reduce_sum.42
  (6 shorter events, 0.1 us)
Async XLA Ops:
  0.0 247.2 %copy-start = (bf16[128,6144]{1,0:T(8,128)(2,1)S(1)}, bf16[128,6144]{1,0:T(8,128)(2,1)}, u32[]{:S(2)}) copy-start(bf16[128,6144]{1,0:T(8,128)(2,1)} %param.11) | copy-start | bytes 4718596
  242.9 3.2 copy-start.2
  244.1 1.9 copy-start.1
  244.1 3.1 copy-start.3
  262.3 6.8 %copy-start.4 = (f32[32,2]{0,1:T(2,128)S(1)}, f32[32,2]{0,1:T(2,128)}, u32[]{:S(2)}) copy-start(f32[32,2]{0,1:T(2,128)} %param.8) | copy-start | bytes 772
  262.3 111.8 %all-to-all-start.2 = ((bf16[16,20,6144]{2,1,0:T(8,128)(2,1)}), bf16[16,20,6144]{2,1,0:T(8,128)(2,1)}, u32[]{:S(2)}, u32[]{:S(2)}) async-start(bf16[16,20,6144]{2,1,0:T(8,128)(2,1)} %reshape.33), calls=%async_computation.2 | async-start | bytes 9437184 | tf_op jit(solution)/shard_map/all_to_all | solution.py:68
